TPU v7x, 512 devices: a whole 4x8x8 slice. The times are simulated.
512 devices in a mesh: seq: 64 (over z, y_hi, x), tp: 8 (over y_lo, core).
Axes of the slice: x: 4, y: 8 (y_hi: 2, y_lo: 4; y = y_hi * 4 + y_lo), z: 8, core: 2. Of those that a mesh axis runs over, the one named last changes fastest.
Arguments:
- tokens: bfloat16 [8192, 2048], P('seq', 'tp'), may hold values from -6 to 6
- ln_gain: bfloat16 [2048], replicated, may hold values from 0.5 to 4.1
- w_qkv: bfloat16 [3, 2048, 2048], P(None, None, 'tp'), may hold values from -0.15467961 to 0.15467961
- w_out: bfloat16 [2048, 2048], P('tp'), may hold values from -0.1875 to 0.1875
Outputs:
- mixed: bfloat16 [8192, 2048], P('seq', 'tp')
All inputs are finite; a program needn't handle non-finite values.
Results may differ from a plain program's by a relative error of at most 0.011.
Values may be sent and summed in bfloat16 or wider, within the bound.
No kernel may reach another device: no remote copies, remote signals or barrier semaphores. Data moves between devices by JAX's collectives and lax.ppermute only.
A program may use at most 64 MiB of HBM per device.

v0:
```python
import jax
import jax.numpy as jnp
from jax import lax
from jax.sharding import Mesh
from jax.sharding import PartitionSpec as P

HEAD_DIM = 128
TP = ("tp_0", "tp_1")


def joined_along(tiles, dim):
    lengths = list(tiles.shape[1:])
    lengths[dim] *= tiles.shape[0]
    return jnp.moveaxis(tiles, 0, dim).reshape(lengths)


def all_blocks(shard, axes, turns):
    tiles = shard[None]
    for k in turns:
        tiles = lax.all_gather(tiles, axes[k], axis=0, tiled=True)
    held = [lax.axis_size(axes[k]) for k in reversed(turns)]
    tiles = tiles.reshape(*held, *shard.shape)
    turned = sorted(range(len(turns)), key=lambda place: turns[len(turns) - 1 - place])
    return tiles.transpose(*turned, *range(len(turns), tiles.ndim)).reshape(-1, *shard.shape)


def gathered_by_axis(shard, axes, turns, dim):
    return joined_along(all_blocks(shard, axes, turns), dim)


def split_up(shard, dim, devices):
    before, after = (shard.shape[:dim], shard.shape[dim + 1 :])
    return jnp.moveaxis(shard.reshape(*before, devices, -1, *after), dim, 0)


def summed_on_arrival(shard, axis, dim):
    devices = lax.axis_size(axis)
    tiles = lax.all_to_all(split_up(shard, dim, devices), axis, 0, 0, tiled=True)
    return jnp.sum(tiles.astype(jnp.float32), axis=0)


def attend_block(totals, queries, block_kv, factor):
    running, denoms, accum = totals
    heads_here = queries.shape[1]
    keys_part = block_kv[0].reshape(block_kv.shape[1], heads_here, queries.shape[2])
    vals_part = block_kv[1].reshape(block_kv.shape[1], heads_here, queries.shape[2])
    scores = (
        jnp.einsum("thc,shc->ths", queries, keys_part, preferred_element_type=jnp.float32) * factor
    )
    highest = jnp.maximum(running, jnp.max(scores, axis=2))
    expon = jnp.exp(scores - highest[:, :, None])
    denoms = jnp.sum(expon, axis=2)
    weights = expon.astype(jnp.bfloat16)
    accum = jnp.einsum("ths,shc->thc", weights, vals_part, preferred_element_type=jnp.float32)
    return (highest, denoms, accum)


def start_totals(rows, heads_count):
    return (
        jnp.full((rows, heads_count), -1e30, jnp.float32),
        jnp.zeros((rows, heads_count), jnp.float32),
        jnp.zeros((rows, heads_count, HEAD_DIM), jnp.float32),
    )


def on_device(tokens, ln_gain, w_qkv, w_out):
    tok_rows = tokens.shape[0]
    whole = gathered_by_axis(tokens, TP, (0, 1), 1)
    values = whole.astype(jnp.float32)
    average = jnp.mean(values, axis=1, keepdims=True)
    second = jnp.mean(values * values, axis=1, keepdims=True)
    normed = (
        (values - average)
        * lax.rsqrt(second - average * average + 1e-06)
        * ln_gain.astype(jnp.float32)
    ).astype(jnp.bfloat16)
    projected = jnp.einsum("td,jdc->jtc", normed, w_qkv, preferred_element_type=jnp.float32).astype(
        jnp.bfloat16
    )
    heads_here = w_qkv.shape[2] // HEAD_DIM
    factor = HEAD_DIM ** (-0.5)
    queries = projected[0].reshape(tok_rows, heads_here, HEAD_DIM)
    keys_vals = projected[1:3]
    initial = start_totals(tok_rows, heads_here)
    final = attend_block(
        initial, queries, lax.all_gather(keys_vals, "seq", axis=1, tiled=True), factor
    )
    context = (
        (final[2] / final[1][:, :, None])
        .reshape(tok_rows, heads_here * HEAD_DIM)
        .astype(jnp.bfloat16)
    )
    summed = summed_on_arrival(
        lax.dot_general(
            w_out, context, (((0,), (1,)), ((), ())), preferred_element_type=jnp.float32
        ).astype(jnp.bfloat16),
        TP,
        0,
    )
    return (tokens.astype(jnp.float32) + summed.T).astype(jnp.bfloat16)


def solution(mesh):
    split = Mesh(mesh.devices.reshape(mesh.shape["seq"], 4, 2), ("seq", "tp_0", "tp_1"))
    placed = (P("seq", TP), P(), P(None, None, TP), P(TP, None))
    return jax.shard_map(
        on_device, mesh=split, in_specs=placed, out_specs=P("seq", TP), check_vma=False
    )
```

profile of v0, /device:TPU:1, one launch (start us, length us, event | category | flops | bytes accessed | tf_op | source)
XLA Modules:
  0.0 287.6 jit_solution(10540969496366223831)
XLA Ops:
  6.5 0.0 copy-start
  6.5 0.0 all-gather.3.cloned.1.call-start
  6.5 12.4 %all-gather = bf16[512,256]{1,0:T(8,128)(2,1)S(1)} all-gather(bf16[128,256]{1,0:T(8,128)(2,1)} %param.4), channel_id=2, replica_groups=mesh['seq'=64,'tp_0'=4,'tp_1'=2] {'tp_0'}, dimensions={0}, use_global_device_ids=true | all-gather | bytes 327680 | tf_op jit(solution)/shard_map/all_gather | solution.py:20
  18.9 10.5 %all_gather.10 = bf16[8,128,256]{2,1,0:T(8,128)(2,1)S(1)} all-gather(bf16[4,128,256]{2,1,0:T(8,128)(2,1)S(1)} %bitcast.49), channel_id=1, replica_groups=mesh['seq'=64,'tp_0'=4,'tp_1'=2] {'tp_1'}, dimensions={0}, use_global_device_ids=true | all-gather | bytes 786432 | tf_op jit(solution)/shard_map/all_gather | solution.py:20
  29.4 0.2 convert_reduce_fusion.1
  29.5 0.1 convert_element_type.84
  29.6 0.7 convert_element_type.68
  30.3 0.2 multiply_reduce_fusion
  30.5 1.1 copy.20
  31.6 2.6 copy.21
  34.2 1.6 fusion.19
  35.7 0.0 copy-done
  35.7 0.6 fusion.7
  36.4 0.7 slice.16
  37.0 0.0 all-gather.3.cloned.1.call-update
  37.1 176.1 %all-gather.3.cloned.1.call-done = bf16[2,8192,256]{2,1,0:T(8,128)(2,1)} async-done(((bf16[2,128,256]{2,1,0:T(8,128)(2,1)}), bf16[2,8192,256]{2,1,0:T(8,128)(2,1)}) %all-gather.3.cloned.1.call-update) | async-done | bytes 8388624 | tf_op jit(solution)/shard_map/all_gather | solution.py:86
  213.2 5.7 %fusion.23 = (bf16[1,8192,256]{2,1,0:T(8,128)(2,1)}, bf16[1,8192,256]{2,1,0:T(8,128)(2,1)}) fusion(bf16[2,8192,256]{2,1,0:T(8,128)(2,1)} %all-gather.3.cloned.1.call-done), kind=kLoop, calls=%fused_computation.29 | loop fusion | bytes 16777216 | tf_op jit(solution)/shard_map/slice | solution.py:45
  218.9 6.9 %reshape_squeeze.10 = bf16[8192,2,128]{2,1,0:T(2,128)(2,1)} reshape(bf16[1,8192,256]{2,1,0:T(8,128)(2,1)} %get-tuple-element.5) | data formatting | bytes 8388608 | tf_op jit(solution)/shard_map/reshape;squeeze | solution.py:45
  225.9 6.7 %fusion.24 = (f32[128,2]{0,1:T(2,128)S(1)}, f32[128,2,8192]{0,2,1:T(8,128)}) fusion(bf16[128,2,128]{2,1,0:T(2,128)(2,1)S(1)} %reshape_squeeze.11, bf16[8192,2,128]{2,1,0:T(2,128)(2,1)} %reshape_squeeze.10), kind=kOutput, calls=%fused_computation.30 | convolution fusion | flops 541064960 | bytes 12649472 | tf_op jit(solution)/shard_map/thc,shc->ths/dot_general | solution.py:48
  232.5 6.4 %copy.31 = bf16[1,8192,256]{1,2,0:T(8,128)(2,1)} copy(bf16[1,8192,256]{2,1,0:T(8,128)(2,1)} %get-tuple-element.6) | data formatting | bytes 8388608 | tf_op jit(solution)/shard_map/reshape;squeeze | solution.py:46
  238.9 0.0 copy-start.1
  238.9 4.6 %fusion.1 = f32[128,2]{0,1:T(2,128)S(1)} fusion(f32[128,2,8192]{0,2,1:T(8,128)} %get-tuple-element.10, f32[128,2]{0,1:T(2,128)S(1)} %broadcast_maximum_fusion), kind=kLoop, calls=%fused_computation.3 | loop fusion | flops 4194048 | bytes 8390656 | tf_op jit(solution)/shard_map/reduce_sum | solution.py:52
  243.5 1.1 copy-done.1
  244.7 0.0 copy-start.2
  244.7 4.2 %fusion.14 = bf16[128,2,128]{0,2,1:T(8,128)(2,1)S(1)} fusion(bf16[8192,2,128]{0,2,1:T(8,128)(2,1)} %bitcast.43, f32[128,2,8192]{0,2,1:T(8,128)S(1)} %copy-done.1, f32[128,2]{0,1:T(2,128)S(1)} %broadcast_maximum_fusion, f32[128,2]{0,1:T(2,128)S(1)} %fusion.1), kind=kOutput, calls=%fused_computation.13 | convolution fusion | flops 541130752 | bytes 12650496 | tf_op jit(solution)/shard_map/ths,shc->thc/dot_general | solution.py:54
  248.9 0.0 copy-start.3
  248.9 0.0 copy-done.2
  248.9 0.3 convolution_convert_fusion
  249.3 30.7 %all_to_all.5 = bf16[8,256,128]{1,2,0:T(8,128)(2,1)S(1)} all-to-all(bf16[8,256,128]{1,2,0:T(8,128)(2,1)S(1)} %bitcast.48), channel_id=1, replica_groups=mesh['seq'=64,'tp_0'=4,'tp_1'=2] {'tp_0','tp_1'}, dimensions={0} | all-to-all | bytes 1048576 | tf_op jit(solution)/shard_map/all_to_all | solution.py:38
  280.0 0.1 convert_reduce_fusion
  280.1 0.0 copy-done.3
  280.1 0.6 fusion.21
  (5 shorter events, 0.1 us)
Async XLA Ops:
  6.5 29.2 %copy-start = (bf16[3,2048,256]{2,1,0:T(8,128)(2,1)S(1)}, bf16[3,2048,256]{2,1,0:T(8,128)(2,1)}, u32[]{:S(2)}) copy-start(bf16[3,2048,256]{2,1,0:T(8,128)(2,1)} %param.6) | copy-start | bytes 9437188
  6.5 206.7 %all-gather.3.cloned.1.call-start = ((), (), s32[]{:S(2)}) async-start(), calls=%async_computation.1 | async-start | bytes 8519680 | tf_op jit(solution)/shard_map/all_gather | solution.py:86
  238.9 5.8 %copy-start.1 = (f32[128,2,8192]{0,2,1:T(8,128)S(1)}, f32[128,2,8192]{0,2,1:T(8,128)}, u32[]{:S(2)}) copy-start(f32[128,2,8192]{0,2,1:T(8,128)} %get-tuple-element.10) | copy-start | bytes 25165828
  244.7 4.2 %copy-start.2 = (bf16[256,2048]{1,0:T(8,128)(2,1)S(1)}, bf16[256,2048]{1,0:T(8,128)(2,1)}, u32[]{:S(2)}) copy-start(bf16[256,2048]{1,0:T(8,128)(2,1)} %param.7) | copy-start | bytes 3145732
  248.9 31.2 %copy-start.3 = (bf16[128,256]{1,0:T(8,128)(2,1)S(1)}, bf16[128,256]{1,0:T(8,128)(2,1)}, u32[]{:S(2)}) copy-start(bf16[128,256]{1,0:T(8,128)(2,1)} %param.4) | copy-start | bytes 196612
Sparse Core Ops, SparseCore 0:
  37.2 175.9 all-gather.2
where the time goes:
time: 288 us
  waiting for transfers between devices  176 us (61%)
  blocking collectives  53.6 us (19%)
  local copies, waits for them, and re-layouts  24.6 us (9%)
  between operations  13.5 us (5%)
  matrix products  11.8 us (4%)
  other arithmetic  8.01 us (3%)
    all_gather x1, waiting for transfers between devices, on_device(): lax.all_gather(keys_vals, 'seq', axis=1, tiled=True)  176 us
    all_to_all x1, blocking collectives, summed_on_arrival(): lax.all_to_all(split_up(shard, dim, devices), axis, 0, 0, tiled=True)  30.7 us
    all_gather x2, blocking collectives, all_blocks(): tiles = lax.all_gather(tiles, axes[k], axis=0, tiled=True)  22.8 us
    another operation x1, local copies, waits for them, and re-layouts, attend_block(): block_kv[0].reshape(block_kv.shape[1], heads_here, queries.shape[2])  6.93 us
    dot_general x1, matrix products, attend_block(): jnp.einsum('thc,shc->ths', queries, keys_part, preferred_element_type=jnp...  6.67 us
    another operation x1, local copies, waits for them, and re-layouts, attend_block(): block_kv[1].reshape(block_kv.shape[1], heads_here, queries.shape[2])  6.37 us
  transfers between devices with their start and end apart: 1, of which 1 were waited for; matrix products, arithmetic and copies ran while one was open for 0% of the time, Pallas kernels for 0%

commit v1 on v0

--- a/solution.py
+++ b/solution.py
@@ -6,6 +6,11 @@
 
 HEAD_DIM = 128
 TP = ("tp_0", "tp_1")
+
+
+def swapped_in(x, axis, dim):
+    sent = jnp.stack([x] * lax.axis_size(axis))
+    return jnp.concatenate(lax.all_to_all(sent, axis, 0, 0), axis=dim)
 
 
 def joined_along(tiles, dim):
@@ -82,9 +87,7 @@
     queries = projected[0].reshape(tok_rows, heads_here, HEAD_DIM)
     keys_vals = projected[1:3]
     initial = start_totals(tok_rows, heads_here)
-    final = attend_block(
-        initial, queries, lax.all_gather(keys_vals, "seq", axis=1, tiled=True), factor
-    )
+    final = attend_block(initial, queries, swapped_in(keys_vals, "seq", 1), factor)
     context = (
         (final[2] / final[1][:, :, None])
         .reshape(tok_rows, heads_here * HEAD_DIM)

time: 288 us -> 349 us (1.21)
  the two profiles are of different devices: /device:TPU:1 before, /device:TPU:68 now
where the time goes in v1:
time: 349 us
  waiting for transfers between devices  218 us (62%)
  blocking collectives  50.4 us (14%)
  local copies, waits for them, and re-layouts  39.7 us (11%)
  starting transfers between devices  18.7 us (5%)
  matrix products  13.8 us (4%)
  other arithmetic  8.01 us (2%)
    all_to_all x1, waiting for transfers between devices, swapped_in(): return jnp.concatenate(lax.all_to_all(sent, axis, 0, 0), axis=dim)  218 us
    all_to_all x1, blocking collectives, summed_on_arrival(): lax.all_to_all(split_up(shard, dim, devices), axis, 0, 0, tiled=True)  33.7 us
    all_to_all x1, starting transfers between devices, swapped_in(): return jnp.concatenate(lax.all_to_all(sent, axis, 0, 0), axis=dim)  18.7 us
    all_gather x2, blocking collectives, all_blocks(): tiles = lax.all_gather(tiles, axes[k], axis=0, tiled=True)  16.7 us
    slice x2, local copies, waits for them, and re-layouts, attend_block(): block_kv[0].reshape(block_kv.shape[1], heads_here, queries.shape[2])  9.76 us
    dot_general x1, matrix products, attend_block(): jnp.einsum('thc,shc->ths', queries, keys_part, preferred_element_type=jnp...  7.47 us
    another operation x1, local copies, waits for them, and re-layouts, attend_block(): block_kv[1].reshape(block_kv.shape[1], heads_here, queries.shape[2])  7.3 us
    another operation x1, local copies, waits for them, and re-layouts, attend_block(): block_kv[0].reshape(block_kv.shape[1], heads_here, queries.shape[2])  7.3 us
  transfers between devices with their start and end apart: 1, of which 1 were waited for; matrix products, arithmetic and copies ran while one was open for 0% of the time, Pallas kernels for 0%

profile of v1, /device:TPU:68, one launch (start us, length us, event | category | flops | bytes accessed | tf_op | source)
XLA Modules:
  0.0 348.7 jit_solution(1630205872985902585)
XLA Ops:
  0.0 0.0 copy-start
  0.0 14.5 %all-gather = bf16[512,256]{1,0:T(8,128)(2,1)S(1)} all-gather(bf16[128,256]{1,0:T(8,128)(2,1)} %param.4), channel_id=2, replica_groups=mesh['seq'=64,'tp_0'=4,'tp_1'=2] {'tp_0'}, dimensions={0}, use_global_device_ids=true | all-gather | bytes 327680 | tf_op jit(solution)/shard_map/all_gather | solution.py:25
  14.5 2.2 all_gather.7
  16.7 0.2 convert_reduce_fusion.1
  16.8 0.1 convert_element_type.84
  16.9 0.7 convert_element_type.68
  17.6 0.2 multiply_reduce_fusion
  17.8 1.1 copy.28
  18.8 2.6 copy.29
  21.4 1.6 fusion.18
  23.0 0.0 copy-done
  23.0 0.6 fusion.6
  23.7 0.6 slice.18
  24.3 1.0 copy.31
  25.3 5.3 %stack.2 = bf16[64,2,128,256]{2,3,1,0:T(8,128)(2,1)} broadcast(bf16[2,128,256]{1,2,0:T(8,128)(2,1)S(1)} %copy.31), dimensions={1,2,3} | broadcast | bytes 8519680 | tf_op jit(solution)/shard_map/stack | solution.py:12
  30.6 18.7 %all-to-all-start = ((bf16[64,2,128,256]{2,3,1,0:T(8,128)(2,1)}), bf16[64,2,128,256]{2,3,1,0:T(8,128)(2,1)}, u32[]{:S(2)}, u32[]{:S(2)}) async-start(bf16[64,2,128,256]{2,3,1,0:T(8,128)(2,1)} %stack.2), calls=%async_computation | async-start | bytes 16777216 | tf_op jit(solution)/shard_map/all_to_all | solution.py:13
  49.4 218.0 %all-to-all-done = bf16[64,2,128,256]{2,3,1,0:T(8,128)(2,1)} async-done(((bf16[64,2,128,256]{2,3,1,0:T(8,128)(2,1)}), bf16[64,2,128,256]{2,3,1,0:T(8,128)(2,1)}, u32[]{:S(2)}, u32[]{:S(2)}) %all-to-all-start) | async-done | bytes 8388640 | tf_op jit(solution)/shard_map/all_to_all | solution.py:13
  267.3 5.1 %fusion.22 = (bf16[1,64,128,256]{2,3,0,1:T(8,128)(2,1)S(1)}, bf16[1,64,128,256]{2,3,0,1:T(8,128)(2,1)}) fusion(bf16[2,64,128,256]{2,3,0,1:T(8,128)(2,1)} %bitcast.8), kind=kLoop, calls=%fused_computation.28 | loop fusion | bytes 16777216 | tf_op jit(solution)/shard_map/slice | solution.py:50
  272.5 4.6 %copy.33 = bf16[1,64,128,256]{2,1,3,0:T(8,128)(2,1)} copy(bf16[1,64,128,256]{2,3,0,1:T(8,128)(2,1)S(1)} %get-tuple-element.5) | data formatting | bytes 8388608 | tf_op jit(solution)/shard_map/slice | solution.py:50
  277.1 7.3 %reshape_squeeze.10 = bf16[8192,2,128]{0,2,1:T(8,128)(2,1)} reshape(bf16[1,64,128,256]{2,1,3,0:T(8,128)(2,1)} %copy.33) | data formatting | bytes 8388608 | tf_op jit(solution)/shard_map/reshape;squeeze | solution.py:50
  284.4 7.5 %fusion.23 = (f32[128,2]{0,1:T(2,128)S(1)}, f32[128,2,8192]{0,2,1:T(8,128)}) fusion(bf16[8192,2,128]{0,2,1:T(8,128)(2,1)} %reshape_squeeze.10, bf16[128,2,128]{2,1,0:T(2,128)(2,1)S(1)} %reshape_squeeze.11), kind=kOutput, calls=%fused_computation.29 | convolution fusion | flops 541064960 | bytes 12649472 | tf_op jit(solution)/shard_map/thc,shc->ths/dot_general | solution.py:53
  291.9 4.7 %copy.32 = bf16[1,64,128,256]{2,1,3,0:T(8,128)(2,1)} copy(bf16[1,64,128,256]{2,3,0,1:T(8,128)(2,1)S(1)} %copy-done.2) | data formatting | bytes 8388608 | tf_op jit(solution)/shard_map/slice | solution.py:51
  296.6 7.3 %reshape_squeeze.9 = bf16[8192,2,128]{0,2,1:T(8,128)(2,1)} reshape(bf16[1,64,128,256]{2,1,3,0:T(8,128)(2,1)} %copy.32) | data formatting | bytes 8388608 | tf_op jit(solution)/shard_map/reshape;squeeze | solution.py:51
  303.9 4.6 %fusion.1 = f32[128,2]{0,1:T(2,128)S(1)} fusion(f32[128,2,8192]{0,2,1:T(8,128)} %get-tuple-element.10, f32[128,2]{0,1:T(2,128)S(1)} %broadcast_maximum_fusion), kind=kLoop, calls=%fused_computation.3 | loop fusion | flops 4194048 | bytes 8390656 | tf_op jit(solution)/shard_map/reduce_sum | solution.py:57
  308.5 0.0 copy-start.3
  308.5 5.4 %fusion.13 = bf16[128,2,128]{0,2,1:T(8,128)(2,1)S(1)} fusion(bf16[8192,2,128]{0,2,1:T(8,128)(2,1)S(1)} %copy-done.1, f32[128,2,8192]{0,2,1:T(8,128)} %get-tuple-element.10, f32[128,2]{0,1:T(2,128)S(1)} %broadcast_maximum_fusion, f32[128,2]{0,1:T(2,128)S(1)} %fusion.1), kind=kOutput, calls=%fused_computation.12 | convolution fusion | flops 541130752 | bytes 12650496 | tf_op jit(solution)/shard_map/ths,shc->thc/dot_general | solution.py:59
  313.9 0.0 copy-start.4
  313.9 0.0 copy-done.3
  313.9 0.3 convolution_convert_fusion
  314.3 33.7 %all_to_all.10 = bf16[8,256,128]{1,2,0:T(8,128)(2,1)S(1)} all-to-all(bf16[8,256,128]{1,2,0:T(8,128)(2,1)S(1)} %bitcast.56), channel_id=1, replica_groups=mesh['seq'=64,'tp_0'=4,'tp_1'=2] {'tp_0','tp_1'}, dimensions={0} | all-to-all | bytes 1048576 | tf_op jit(solution)/shard_map/all_to_all | solution.py:43
  348.0 0.1 convert_reduce_fusion
  348.1 0.6 fusion.20
  (10 shorter events, 0.1 us)
Async XLA Ops:
  0.0 23.0 %copy-start = (bf16[3,2048,256]{2,1,0:T(8,128)(2,1)S(1)}, bf16[3,2048,256]{2,1,0:T(8,128)(2,1)}, u32[]{:S(2)}) copy-start(bf16[3,2048,256]{2,1,0:T(8,128)(2,1)} %param.6) | copy-start | bytes 9437188
  30.6 236.7 %all-to-all-start = ((bf16[64,2,128,256]{2,3,1,0:T(8,128)(2,1)}), bf16[64,2,128,256]{2,3,1,0:T(8,128)(2,1)}, u32[]{:S(2)}, u32[]{:S(2)}) async-start(bf16[64,2,128,256]{2,3,1,0:T(8,128)(2,1)} %stack.2), calls=%async_computation | async-start | bytes 16777216 | tf_op jit(solution)/shard_map/all_to_all | solution.py:13
  284.4 7.5 %copy-start.2 = (bf16[1,64,128,256]{2,3,0,1:T(8,128)(2,1)S(1)}, bf16[1,64,128,256]{2,3,0,1:T(8,128)(2,1)}, u32[]{:S(2)}) copy-start(bf16[1,64,128,256]{2,3,0,1:T(8,128)(2,1)} %get-tuple-element.6) | copy-start | bytes 12582916
  303.9 4.6 %copy-start.1 = (bf16[8192,2,128]{0,2,1:T(8,128)(2,1)S(1)}, bf16[8192,2,128]{0,2,1:T(8,128)(2,1)}, u32[]{:S(2)}) copy-start(bf16[8192,2,128]{0,2,1:T(8,128)(2,1)} %reshape_squeeze.9) | copy-start | bytes 12582916
  308.5 5.4 %copy-start.3 = (bf16[256,2048]{1,0:T(8,128)(2,1)S(1)}, bf16[256,2048]{1,0:T(8,128)(2,1)}, u32[]{:S(2)}) copy-start(bf16[256,2048]{1,0:T(8,128)(2,1)} %param.7) | copy-start | bytes 3145732
  313.9 34.2 %copy-start.4 = (bf16[128,256]{1,0:T(8,128)(2,1)S(1)}, bf16[128,256]{1,0:T(8,128)(2,1)}, u32[]{:S(2)}) copy-start(bf16[128,256]{1,0:T(8,128)(2,1)} %param.4) | copy-start | bytes 196612
